TPU v7x, 32 devices: a whole 2x2x4 slice. The times are simulated.
32 devices in a mesh: dp: 8 (over y, x, core), tensor: 4 (over z).
Axes of the slice: x: 2, y: 2, z: 4, core: 2. Of those that a mesh axis runs over, the one named last changes fastest.
Arguments:
- acts: bfloat16 [1024, 4096], P('dp'), may hold values from -6 to 6
- grad_out: bfloat16 [1024, 14336], P('dp', 'tensor'), may hold values from -0.1875 to 0.1875
- selected: int32 [4, 4], P('tensor'), may hold values from 0 to 27, as said below
- owner: int32 [4, 192, 1], P('tensor'), may hold values from 0 to 7; in each aligned block of 192 rows (0 to 191, 192 to 383, ..., all dimensions but the last counted through in order) at most 36 rows name the same one
- sel_weight: float32 [4096, 2048], P('dp', 'tensor'), may hold values from -3 to 3
- sel_moment: float32 [4096, 2048], P('dp', 'tensor'), may hold values from -3 to 3
- sel_second: float32 [4096, 2048], P('dp', 'tensor'), may hold values from 0.01 to 1
- off_weight: float32 [8, 4, 36, 512, 128], P('dp', 'tensor'), may hold values from -3 to 3
- off_moment: float32 [8, 4, 36, 512, 128], P('dp', 'tensor'), may hold values from -3 to 3
- off_second: float32 [8, 4, 36, 512, 128], P('dp', 'tensor'), may hold values from 0.01 to 1
Outputs:
- column_norm: float32 [14336], P('tensor')
- sel_weight_new: float32 [4096, 2048], P('dp', 'tensor')
- sel_moment_new: float32 [4096, 2048], P('dp', 'tensor')
- sel_second_new: float32 [4096, 2048], P('dp', 'tensor')
- off_weight_new: float32 [8, 4, 36, 512, 128], P('dp', 'tensor')
- off_moment_new: float32 [8, 4, 36, 512, 128], P('dp', 'tensor')
- off_second_new: float32 [8, 4, 36, 512, 128], P('dp', 'tensor')
Inputs may be any that keep to these rules, and one draw needn't show every extreme that they name: `selected`: each row names 4 tile. For each index of tensor, no owner receives more than 36 pieces, and some owner receives exactly 36.
All inputs are finite; a program needn't handle non-finite values.
Results may differ from a plain program's by a relative error of at most 0.0017.
Values may be sent and summed in bfloat16 or wider, within the bound.
A program may use at most 192 MiB of HBM per device.

v0:
```python
import functools

import jax
import jax.numpy as jnp
from jax import lax
from jax.experimental import pallas as pl
from jax.experimental.pallas import tpu as pltpu
from jax.sharding import PartitionSpec as P

TILE = 128
VMEM_LIMIT = 56 * 1024 * 1024


beta_one = 0.9
beta_two = 0.95
adam_eps = 1e-08
learn_rate = 0.01
decay_rate = 0.1
step_count = 10.0


def adam_update(weight, moment, second, grad):
    moment_new = beta_one * moment + (1.0 - beta_one) * grad
    second_new = beta_two * second + (1.0 - beta_two) * grad * grad
    first_fix = 1.0 - beta_one**step_count
    second_fix = 1.0 - beta_two**step_count
    update = moment_new / first_fix / (jnp.sqrt(second_new / second_fix) + adam_eps)
    return (weight - learn_rate * (update + decay_rate * weight), moment_new, second_new)


MESH = pl.DeviceIdType.MESH


def flip_bits(index, mask):
    result, bit = index, 1
    while bit <= mask:
        if mask & bit:
            result = result + bit * (1 - 2 * ((index // bit) % 2))
        bit *= 2
    return result


def gather_kernel(
    n,
    paired,
    tile_slot,
    block_slot,
    sel_tile,
    acts,
    acts_t,
    grad,
    offload,
    sel_sum,
    norm,
    total,
    squares,
    send_sem,
    recv_a,
    recv_z,
    recv_g,
    recv_e,
    send_q,
    recv_q,
    *held,
):
    held_a, held_g = (acts_t,) + held[: n - 1], (grad,) + held[n - 1 :]
    layer = lax.axis_index("tensor")
    half, cut = n // 2, grad.shape[0] * 3 // 4
    side = layer % 2
    parts = {
        "a": (held_a, pl.ds(side * half, half), recv_a),
        "z": (held_a, pl.ds((1 - side) * half, half), recv_z),
        "g": (held_g, pl.ds(0, cut), recv_g),
        "e": (held_g, pl.ds(cut, grad.shape[0] - cut), recv_e),
    }
    me = lax.axis_index("dp")
    capacity = offload.shape[0]
    sel_count = sel_tile.shape[0]
    rows_all = acts.shape[1]

    barrier = pltpu.get_barrier_semaphore()
    for mask in range(1, n):
        pl.semaphore_signal(
            barrier, inc=1, device_id={"dp": flip_bits(me, mask)}, device_id_type=MESH
        )
    if paired:
        pl.semaphore_signal(
            barrier, inc=1, device_id={"tensor": flip_bits(layer, 1)}, device_id_type=MESH
        )
    pl.semaphore_wait(barrier, n if paired else n - 1)

    started = []

    def part_of(kind, mask):
        slots, place, _ = parts[kind]
        return slots[mask].at[place]

    def copy_of(kind, mask, peer, number):
        there = mask ^ peer
        return pltpu.make_async_remote_copy(
            src_ref=part_of(kind, mask),
            dst_ref=part_of(kind, there),
            send_sem=send_sem.at[number],
            recv_sem=parts[kind][2].at[there - 1],
            device_id={"dp": flip_bits(me, peer)},
            device_id_type=MESH,
        )

    def send_across(mask):
        part = part_of("a", mask)
        copy = pltpu.make_async_remote_copy(
            src_ref=part,
            dst_ref=part,
            send_sem=send_sem.at[len(started)],
            recv_sem=recv_z.at[mask - 1],
            device_id={"tensor": flip_bits(layer, 1)},
            device_id_type=MESH,
        )
        copy.start()
        started.append(copy)

    def send(kind, mask, peer):
        copy = copy_of(kind, mask, peer, len(started))
        copy.start()
        started.append(copy)

    def arrived(kind, mask):
        copy_of(kind, 0, mask, 0).wait_recv()

    def square_columns():
        gram = jnp.dot(
            acts[...], acts_t[...].reshape(rows_all, -1), preferred_element_type=jnp.float32
        )
        high = gram.astype(jnp.bfloat16)
        rest = gram - high.astype(jnp.float32)
        middle = rest.astype(jnp.bfloat16)
        low = (rest - middle.astype(jnp.float32)).astype(jnp.bfloat16)

        @pl.loop(0, grad.shape[0])
        def _(tile):
            piece = grad[tile]
            product = jnp.dot(low, piece, preferred_element_type=jnp.float32)
            product += jnp.dot(middle, piece, preferred_element_type=jnp.float32)
            product += jnp.dot(high, piece, preferred_element_type=jnp.float32)
            squares[0, tile] = jnp.sum(
                piece.astype(jnp.float32) * product, axis=0, keepdims=True
            )

    def square_copy(mask):
        return pltpu.make_async_remote_copy(
            src_ref=squares.at[0],
            dst_ref=squares.at[mask],
            send_sem=send_q.at[mask - 1],
            recv_sem=recv_q.at[mask - 1],
            device_id={"dp": flip_bits(me, mask)},
            device_id_type=MESH,
        )

    def add_blocks(masks, first, last):
        def product(mask, block, tile):
            return jnp.dot(
                held_a[mask][block], held_g[mask][tile], preferred_element_type=jnp.float32
            )

        @pl.loop(0, capacity)
        def _(slot):
            block, tile = block_slot[slot], tile_slot[slot]
            value = None if first else total[slot]
            for mask in masks:
                part = product(mask, block, tile)
                part = part.astype(jnp.bfloat16).astype(jnp.float32)
                value = part if value is None else value + part
            if last:
                offload[slot] = value.astype(jnp.bfloat16)
            else:
                total[slot] = value

        for i in range(sel_count):
            tile = sel_tile[i]
            place = pl.ds(i * TILE, TILE)
            value = None if first else sel_sum[:, place]
            for mask in masks:
                part = product(mask, me, tile)
                value = part if value is None else value + part
            sel_sum[:, place] = value

    def relay(kinds, mask):
        for kind in kinds:
            arrived(kind, mask)
            send(kind, mask, 1)

    def complete(mask):
        for kind in parts:
            arrived(kind, mask)

    def send_squares():
        for mask in range(1, n):
            square_copy(mask).start()

    if paired:
        core, near, far = 1, 2, 4
        both = near ^ far
        send("a", 0, near)
        send("a", 0, far)
        send("g", 0, near)
        send("g", 0, far)
        send("e", 0, far)
        for kind in parts:
            send(kind, 0, core)
        square_columns()
        arrived("a", far)
        send("a", far, near)
        send("e", 0, near)
        send_across(far)
        send("a", far, core)
        arrived("a", near)
        send_across(near)
        send("a", near, core)
        complete(core)
        add_blocks((0, core), True, False)
        send_squares()
        relay("z", far)
        arrived("g", near)
        send("g", near, far)
        send("g", near, core)
        arrived("e", far)
        send("e", far, near)
        send("e", far, core)
        relay("g", far)
        add_blocks((far,), False, False)
        arrived("a", both)
        send_across(both)
        send("a", both, core)
        relay("z", near)
        complete(far ^ core)
        add_blocks((far ^ core,), False, False)
        relay("e", near)
        complete(near ^ core)
        add_blocks((near, near ^ core), False, False)
        relay("gez", both)
        complete(both ^ core)
        add_blocks((both, both ^ core), False, True)
    else:
        for mask in range(1, n):
            for kind in parts:
                send(kind, 0, mask)
        square_columns()
        add_blocks((0,), True, False)
        send_squares()
        for mask in range(1, n):
            complete(mask)
            add_blocks((mask,), False, mask == n - 1)

    whole = squares[0]
    for mask in range(1, n):
        square_copy(mask).wait_recv()
        whole = whole + squares[mask]
    norm[...] = jnp.sqrt(whole)
    for copy in started:
        copy.wait_send()
    for mask in range(1, n):
        square_copy(mask).wait_send()


def body(
    acts,
    grad_out,
    selected,
    owner,
    sel_weight,
    sel_moment,
    sel_second,
    off_weight,
    off_moment,
    off_second,
):
    n = lax.axis_size("dp")
    tokens_here, rows_all = acts.shape
    cols_here = grad_out.shape[1]
    tiles_here = cols_here // TILE
    sel_count = selected.shape[1]
    rest_count = tiles_here - sel_count
    row_block = rows_all // n
    capacity = off_weight.shape[2]
    piece_count = rest_count * n
    selected_row = selected[0]
    owner_row = owner[0, :, 0]
    mine = (owner_row == lax.axis_index("dp")).astype(jnp.int32)
    pieces = jnp.arange(piece_count, dtype=jnp.int32)
    before = jnp.sum(mine[None, :] * (pieces[:, None] > pieces[None, :]), axis=1)
    taken = mine[None, :] * (before[None, :] == jnp.arange(capacity)[:, None])
    piece = jnp.sum(taken * pieces[None, :], axis=1)
    filled = jnp.sum(taken, axis=1) > 0
    order = piece // n
    tiles = jnp.arange(tiles_here, dtype=jnp.int32)
    free = 1 - jnp.any(tiles[:, None] == selected_row[None, :], axis=1).astype(jnp.int32)
    rank = jnp.sum(free[None, :] * (tiles[:, None] > tiles[None, :]), axis=1)
    named = free[None, :] * (rank[None, :] == order[:, None])
    tile_slot = jnp.sum(named * tiles[None, :], axis=1).astype(jnp.int32)
    block_slot = (piece % n).astype(jnp.int32)

    acts_t = acts.T.reshape(n, row_block, tokens_here)
    grad_tiles = jnp.moveaxis(grad_out.reshape(tokens_here, tiles_here, TILE), 1, 0)
    paired = n == 8 and lax.axis_size("tensor") % 2 == 0
    sends = 28 if paired else 4 * (n - 1)
    in_vmem = pl.BlockSpec(memory_space=pltpu.VMEM)
    in_smem = pl.BlockSpec(memory_space=pltpu.SMEM)
    offload, sel_sum, norm = pl.pallas_call(
        functools.partial(gather_kernel, n, paired),
        out_shape=(
            jax.ShapeDtypeStruct((capacity, row_block, TILE), jnp.bfloat16),
            jax.ShapeDtypeStruct((row_block, sel_count * TILE), jnp.float32),
            jax.ShapeDtypeStruct((tiles_here, 1, TILE), jnp.float32),
        ),
        in_specs=[in_smem] * 3 + [in_vmem] * 3,
        out_specs=(in_vmem,) * 3,
        scratch_shapes=[
            pltpu.VMEM((capacity, row_block, TILE), jnp.float32),
            pltpu.VMEM((n, tiles_here, 1, TILE), jnp.float32),
            pltpu.SemaphoreType.DMA((sends,)),
            pltpu.SemaphoreType.DMA((n - 1,)),
            pltpu.SemaphoreType.DMA((n - 1,)),
            pltpu.SemaphoreType.DMA((n - 1,)),
            pltpu.SemaphoreType.DMA((n - 1,)),
            pltpu.SemaphoreType.DMA((n - 1,)),
            pltpu.SemaphoreType.DMA((n - 1,)),
        ]
        + [pltpu.VMEM((n, row_block, tokens_here), jnp.bfloat16)] * (n - 1)
        + [pltpu.VMEM((tiles_here, tokens_here, TILE), jnp.bfloat16)] * (n - 1),
        compiler_params=pltpu.CompilerParams(
            collective_id=0, has_side_effects=True, vmem_limit_bytes=VMEM_LIMIT
        ),
    )(tile_slot, block_slot, selected_row, acts, acts_t, grad_tiles)
    new_sel = adam_update(sel_weight, sel_moment, sel_second, sel_sum)
    zero_half = jnp.zeros((), jnp.bfloat16)
    off_grad = jnp.where(filled[:, None, None], offload, zero_half).astype(jnp.float32)
    new_off = adam_update(
        off_weight, off_moment, off_second, off_grad.reshape(off_weight.shape)
    )
    return (norm.reshape(cols_here), *new_sel, *new_off)


def solution(mesh):
    placed = (
        P("dp", None),
        P("dp", "tensor"),
        P("tensor", None),
        P("tensor", None, None),
        P("dp", "tensor"),
        P("dp", "tensor"),
        P("dp", "tensor"),
        P("dp", "tensor", None, None, None),
        P("dp", "tensor", None, None, None),
        P("dp", "tensor", None, None, None),
    )
    return jax.shard_map(
        body,
        mesh=mesh,
        in_specs=placed,
        out_specs=(
            P("tensor"),
            P("dp", "tensor"),
            P("dp", "tensor"),
            P("dp", "tensor"),
            P("dp", "tensor", None, None, None),
            P("dp", "tensor", None, None, None),
            P("dp", "tensor", None, None, None),
        ),
        check_vma=False,
    )
```

profile of v0, /device:TPU:0, one launch (start us, length us, event | category | flops | bytes accessed | tf_op | source)
XLA Modules:
  0.0 111.1 jit_solution(9246458055383846923)
XLA Ops:
  0.6 0.7 compare_convert_fusion
  1.3 0.1 select_reduce_fusion
  1.4 0.1 select_reduce_fusion.1
  1.6 0.5 and_select_fusion
  2.1 0.7 fusion.6
  2.8 0.1 select_reduce_fusion.2
  3.0 0.6 multiply_reduce_fusion.tile_slot
  3.6 1.5 %copy.22 = bf16[128,3584]{0,1:T(8,128)(2,1)S(1)} copy(bf16[128,3584]{1,0:T(8,128)(2,1)} %param.11) | data formatting | bytes 1835008 | tf_op args[1]
  5.1 1.3 %copy.23 = bf16[128,28,128]{2,0,1:T(8,128)(2,1)} copy(bf16[128,28,128]{0,2,1:T(8,128)(2,1)S(1)} %bitcast.19) | data formatting | bytes 1835008 | tf_op jit(solution)/shard_map/reshape | solution.py:303
  6.4 2.3 %copy.21 = bf16[4096,128]{1,0:T(8,128)(2,1)} copy(bf16[4096,128]{0,1:T(8,128)(2,1)} %bitcast.17) | data formatting | bytes 2097152 | tf_op jit(solution)/shard_map/transpose | solution.py:302
  8.7 76.1 %shard_map.153 = (bf16[36,512,128]{2,1,0:T(8,128)(2,1)}, f32[512,512]{1,0:T(8,128)}, f32[28,1,128]{2,1,0:T(1,128)}) custom-call(s32[36]{0:T(128)} %multiply_reduce_fusion.tile_slot, s32[36]{0:T(128)} %get-tuple-element.21.block_slot, s32[4]{0:T(128)} %bitcast.25, bf16[128,4096]{1,0:T(8,128)(2,1)} %acts.1, bf16[8,512,128]{2,1,0:T(8,128)(2,1)} %bitcast.18, ...), custom_call_target="tpu_custom_call" | custom-call | tf_op jit(solution)/shard_map/pallas_call | solution.py:308
  84.8 0.0 copy-start
  84.8 0.0 copy-start.1
  84.8 0.0 copy-start.2
  84.8 0.0 copy-start.3
  84.8 0.0 copy-start.4
  84.8 23.4 %multiply_subtract_fusion = (f32[1,1,36,512,128]{4,3,2,1,0:T(8,128)}, f32[1,1,36,512,128]{4,3,2,1,0:T(8,128)}, f32[1,1,36,512,128]{4,3,2,1,0:T(8,128)}) fusion(f32[1,1,36,512,128]{4,3,2,1,0:T(8,128)} %param.17, bf16[36,512,128]{2,1,0:T(8,128)(2,1)} %get-tuple-element.12, pred[36]{0:T(512)(128)(4,1)S(1)} %broadcast_compare_fusion, ...), kind=kLoop, calls=%fused_computation.6 | loop fusion | flops 40108032 | bytes 61341732 | tf_op jit(solution)/shard_map/sub | solution.py:28
  108.2 0.0 copy-done
  108.2 0.0 copy-done.1
  108.2 0.0 copy-done.2
  108.2 0.0 copy-done.3
  108.2 2.3 %multiply_subtract_fusion.1 = (f32[512,512]{1,0:T(8,128)}, f32[512,512]{1,0:T(8,128)}, f32[512,512]{1,0:T(8,128)}) fusion(f32[512,512]{1,0:T(8,128)S(1)} %copy-done, f32[512,512]{1,0:T(8,128)S(1)} %copy-done.3, f32[512,512]{1,0:T(8,128)S(1)} %copy-done.1, f32[512,512]{1,0:T(8,128)S(1)} %copy-done.2), kind=kLoop, calls=%fused_computation.10 | loop fusion | flops 3932160 | bytes 7340032 | tf_op jit(solution)/shard_map/sub | solution.py:28
  110.5 0.0 copy-done.4
  110.5 0.6 reduce
  (2 shorter events, 0.0 us)
Async XLA Ops:
  84.8 23.4 %copy-start = (f32[512,512]{1,0:T(8,128)S(1)}, f32[512,512]{1,0:T(8,128)}, u32[]{:S(2)}) copy-start(f32[512,512]{1,0:T(8,128)} %param.14) | copy-start | bytes 3145732
  84.8 23.4 %copy-start.1 = (f32[512,512]{1,0:T(8,128)S(1)}, f32[512,512]{1,0:T(8,128)}, u32[]{:S(2)}) copy-start(f32[512,512]{1,0:T(8,128)} %param.15) | copy-start | bytes 3145732
  84.8 23.4 %copy-start.2 = (f32[512,512]{1,0:T(8,128)S(1)}, f32[512,512]{1,0:T(8,128)}, u32[]{:S(2)}) copy-start(f32[512,512]{1,0:T(8,128)} %param.16) | copy-start | bytes 3145732
  84.8 23.4 %copy-start.3 = (f32[512,512]{1,0:T(8,128)S(1)}, f32[512,512]{1,0:T(8,128)}, u32[]{:S(2)}) copy-start(f32[512,512]{1,0:T(8,128)} %get-tuple-element.11) | copy-start | bytes 3145732
  84.8 25.7 %copy-start.4 = (f32[28,1,128]{2,1,0:T(1,128)S(1)}, f32[28,1,128]{2,1,0:T(1,128)}, u32[]{:S(2)}) copy-start(f32[28,1,128]{2,1,0:T(1,128)} %get-tuple-element.10) | copy-start | bytes 43012
where the time goes:
time: 111 us
  Pallas kernels  76.1 us (69%)
  other arithmetic  29.2 us (26%)
  local copies, waits for them, and re-layouts  5.11 us (5%)
    pallas_call x1, Pallas kernels, body(): pl.pallas_call(functools.partial(gather_kernel, n, paired), out_shape=(ja...  76.1 us
    sub x2, other arithmetic, adam_update(): weight - learn_rate * (update + decay_rate * weight)  25.6 us
    transpose x1, local copies, waits for them, and re-layouts, body(): acts_t = acts.T.reshape(n, row_block, tokens_here)  2.26 us

commit v1 on v0

v1 whole, which is shorter than its diff:
```python
import functools

import jax
import jax.numpy as jnp
from jax import lax
from jax.experimental import pallas as pl
from jax.experimental.pallas import tpu as pltpu
from jax.sharding import PartitionSpec as P

TILE = 128
DEPTH = 4
ROWS_ONCE = 128
MIB = 1024 * 1024

beta_one = 0.9
beta_two = 0.95
adam_eps = 1e-08
learn_rate = 0.01
decay_rate = 0.1
step_count = 10.0

MESH = pl.DeviceIdType.MESH


def adam_update(weight, moment, second, grad):
    first_fix = 1.0 - beta_one**step_count
    second_fix = 1.0 - beta_two**step_count
    moment_new = beta_one * moment + (1.0 - beta_one) * grad
    second_new = beta_two * second + (1.0 - beta_two) * (grad * grad)
    scale = jnp.sqrt(second_new * (1.0 / second_fix)) + adam_eps
    update = moment_new * (learn_rate / first_fix) / scale
    return weight * (1.0 - learn_rate * decay_rate) - update, moment_new, second_new


def flip_bits(index, mask):
    result, bit = index, 1
    while bit <= mask:
        if mask & bit:
            result = result + bit * (1 - 2 * ((index // bit) % 2))
        bit *= 2
    return result


def rounded(value):
    return value.astype(jnp.bfloat16).astype(jnp.float32)


def in_hbm(array):
    return pltpu.with_memory_space_constraint(array, pltpu.HBM)


def unroll_of(count):
    return next(k for k in (3, 2, 1) if count % k == 0)


def table_kernel(
    n, capacity, sel_tile, owner, table, next_piece, next_free, rest_tile
):
    me = lax.axis_index("dp")
    sel_count = sel_tile.shape[0]
    piece_count, tiles_here = owner.shape[0], next_free.shape[0] - 1

    def piece_step(i, following):
        p = piece_count - 1 - i
        following = jnp.where(owner[p] == me, p, following)
        next_piece[p] = following
        return following

    next_piece[piece_count] = piece_count
    next_piece[piece_count + 1] = piece_count
    lax.fori_loop(0, piece_count, piece_step, jnp.int32(piece_count))

    def free_step(i, following):
        t = tiles_here - 1 - i
        taken = jnp.int32(0)
        for k in range(sel_count):
            taken = taken + (sel_tile[k] == t).astype(jnp.int32)
        following = jnp.where(taken == 0, t, following)
        next_free[t] = following
        return following

    next_free[tiles_here] = 0
    lax.fori_loop(0, tiles_here, free_step, jnp.int32(0))

    def rest_step(k, at):
        tile = next_free[at]
        rest_tile[k] = tile
        return tile + 1

    lax.fori_loop(0, tiles_here - sel_count, rest_step, jnp.int32(0))

    def slot_step(s, at):
        p = next_piece[at]
        found = p < piece_count
        piece = jnp.where(found, p, 0)
        table[s] = rest_tile[lax.div(piece, n)]
        table[capacity + s] = lax.rem(piece, n)
        table[2 * capacity + s] = found.astype(jnp.int32)
        return p + 1 - (p // piece_count)

    lax.fori_loop(0, capacity, slot_step, jnp.int32(0))
    for k in range(sel_count):
        table[3 * capacity + k] = sel_tile[k]


def gather_kernel(n, paired, late, table_source, acts, grad, *refs):
    states, refs = refs[:5], refs[5:]
    late_a, late_g = refs[: len(late)], refs[len(late) : 2 * len(late)]
    refs = refs[2 * len(late) :]
    kept = refs[:5]
    total, sel_sum, norm = refs[5:8]
    early = [mask for mask in range(n) if mask not in late]
    refs = refs[8:]
    table, raw, squares = refs[:3]
    send_sem, recv_sem, send_q, recv_q, load_sem, grad_sem = refs[3:9]
    held_a = dict(zip(early, refs[9 : 9 + len(early)])) | dict(zip(late, late_a))
    held_g = dict(zip(early, refs[9 + len(early) :])) | dict(zip(late, late_g))

    layer = lax.axis_index("tensor")
    me = lax.axis_index("dp")
    capacity = total.shape[0]
    sel_count = sel_sum.shape[1] // TILE
    row_block = total.shape[1]
    tiles_here = grad.shape[1] // TILE
    kinds = ("a0", "a1", "z0", "z1", "g0", "g1")
    if paired:
        side, part = layer % 2, n // 4
        cut = tiles_here // 2
        parts = {
            "a0": (held_a, (pl.ds(side * 2 * part, part),)),
            "a1": (held_a, (pl.ds(side * 2 * part + part, part),)),
            "z0": (held_a, (pl.ds((1 - side) * 2 * part, part),)),
            "z1": (held_a, (pl.ds((1 - side) * 2 * part + part, part),)),
            "g0": (held_g, (pl.ds(0, cut),)),
            "g1": (held_g, (pl.ds(cut, tiles_here - cut),)),
        }
    else:
        parts = {
            "a0": (held_a, (slice(None),)),
            "g0": (held_g, (slice(None),)),
        }

    own_acts = pltpu.make_async_copy(acts, raw, load_sem.at[0])
    own_table = pltpu.make_async_copy(table_source, table, load_sem.at[1])
    own_grads = [
        pltpu.make_async_copy(
            grad.at[:, pl.ds(tile * TILE, TILE)], held_g[0].at[tile], grad_sem.at[tile]
        )
        for tile in range(tiles_here)
    ]
    own_acts.start()
    own_table.start()
    for copy in own_grads:
        copy.start()
    loads = []
    for number, (source, target) in enumerate(zip(states, kept)):
        load = pltpu.make_async_copy(source, target, load_sem.at[2 + number])
        loads.append(load)

    barrier = pltpu.get_barrier_semaphore()
    for mask in range(1, n):
        pl.semaphore_signal(
            barrier, inc=1, device_id={"dp": flip_bits(me, mask)}, device_id_type=MESH
        )
    if paired:
        pl.semaphore_signal(
            barrier, inc=1, device_id={"tensor": flip_bits(layer, 1)}, device_id_type=MESH
        )
    own_acts.wait()
    for block in range(n):
        held_a[0][block] = raw[:, pl.ds(block * row_block, row_block)].T
    for copy in own_grads:
        copy.wait()
    own_table.wait()
    pl.semaphore_wait(barrier, n if paired else n - 1)

    started = []

    def at_part(kind, mask):
        slots, place = parts[kind]
        return slots[mask].at[place]

    def recv_of(kind, mask):
        return recv_sem.at[kinds.index(kind) * (n - 1) + mask - 1]

    def copy_of(kind, mask, peer, number):
        there = mask ^ peer
        slots, place = parts[kind]
        return pltpu.make_async_remote_copy(
            src_ref=slots[mask].at[place],
            dst_ref=slots[there].at[place],
            send_sem=send_sem.at[number],
            recv_sem=recv_of(kind, there),
            device_id={"dp": flip_bits(me, peer)},
            device_id_type=MESH,
        )

    def send(kind, mask, peer):
        copy = copy_of(kind, mask, peer, len(started))
        copy.start()
        started.append(copy)

    def send_across(kind, mask):
        copy = pltpu.make_async_remote_copy(
            src_ref=at_part(kind, mask),
            dst_ref=at_part(kind, mask),
            send_sem=send_sem.at[len(started)],
            recv_sem=recv_of("z" + kind[1], mask),
            device_id={"tensor": flip_bits(layer, 1)},
            device_id_type=MESH,
        )
        copy.start()
        started.append(copy)

    def arrived(kind, mask):
        copy_of(kind, 0, mask, 0).wait_recv()

    def square_columns():
        whole = held_a[0][...].reshape(n * row_block, raw.shape[0])
        gram = jnp.dot(raw[...], whole, preferred_element_type=jnp.float32)
        high = gram.astype(jnp.bfloat16)
        rest = gram - high.astype(jnp.float32)
        middle = rest.astype(jnp.bfloat16)
        low = (rest - middle.astype(jnp.float32)).astype(jnp.bfloat16)

        @pl.loop(0, tiles_here, unroll=unroll_of(tiles_here))
        def _(tile):
            piece = held_g[0][tile]
            product = jnp.dot(low, piece, preferred_element_type=jnp.float32)
            product += jnp.dot(middle, piece, preferred_element_type=jnp.float32)
            product += jnp.dot(high, piece, preferred_element_type=jnp.float32)
            squares[0, pl.ds(tile, 1)] = jnp.sum(
                piece.astype(jnp.float32) * product, axis=0, keepdims=True
            )

    def square_copy(mask):
        return pltpu.make_async_remote_copy(
            src_ref=squares.at[0],
            dst_ref=squares.at[mask],
            send_sem=send_q.at[mask - 1],
            recv_sem=recv_q.at[mask - 1],
            device_id={"dp": flip_bits(me, mask)},
            device_id_type=MESH,
        )

    def add_slots(masks, first, begin, end):
        @pl.loop(begin, end, unroll=unroll_of(end - begin))
        def _(slot):
            block, tile = table[capacity + slot], table[slot]
            value = None if first else total[slot]
            for mask in masks:
                partial = rounded(
                    jnp.dot(
                        held_a[mask][block],
                        held_g[mask][tile],
                        preferred_element_type=jnp.float32,
                    )
                )
                value = partial if value is None else value + partial
            total[slot] = value

    def add_selected(masks, first):
        for i in range(sel_count):
            tile, place = table[3 * capacity + i], pl.ds(i * TILE, TILE)
            value = None if first else sel_sum[:, place]
            for mask in masks:
                partial = jnp.dot(
                    held_a[mask][me],
                    held_g[mask][tile],
                    preferred_element_type=jnp.float32,
                )
                value = partial if value is None else value + partial
            sel_sum[:, place] = value

    def complete(mask, only=kinds):
        for kind in only:
            if kind in parts:
                arrived(kind, mask)

    def relay(kind, mask):
        arrived(kind, mask)
        send(kind, mask, 1)

    if paired:
        core, near, far = 1, 2, 4
        both = near ^ far
        send("a1", 0, near)
        send("a0", 0, far)
        send("a0", 0, near)
        send("a1", 0, far)
        for kind in kinds:
            send(kind, 0, core)
        for load in loads:
            load.start()
        square_columns()
        for mask in range(1, n):
            square_copy(mask).start()
        relay("a0", far)
        send("a0", far, near)
        send_across("a0", far)
        relay("a1", near)
        send("a1", near, far)
        send_across("a1", near)
        send("g1", 0, near)
        send("g0", 0, far)
        send("g0", 0, near)
        send("g1", 0, far)
        relay("a0", near)
        send_across("a0", near)
        relay("a1", far)
        send_across("a1", far)
        complete(core)
        add_slots((0, core), True, 0, capacity)
        add_selected((0, core), True)
        relay("a0", both)
        send_across("a0", both)
        relay("a1", both)
        send_across("a1", both)
        relay("z0", far)
        relay("z1", near)
        relay("z0", near)
        relay("g0", far)
        send("g0", far, near)
        relay("g1", near)
        send("g1", near, far)
        relay("z1", far)
        relay("g0", near)
        relay("g1", far)
        complete(near ^ core)
        complete(far ^ core)
        middle = (near, near ^ core, far, far ^ core)
        add_slots(middle, False, 0, capacity // 2)
        relay("z0", both)
        relay("z1", both)
        add_slots(middle, False, capacity // 2, capacity)
        add_selected(middle, False)
        relay("g0", both)
        relay("g1", both)
        complete(both ^ core)
    else:
        for mask in range(1, n):
            for kind in parts:
                send(kind, 0, mask)
        for load in loads:
            load.start()
        square_columns()
        for mask in range(1, n):
            square_copy(mask).start()
        add_slots((0,), True, 0, capacity)
        add_selected((0,), True)
        for mask in range(1, n):
            complete(mask)
            if mask not in late:
                add_slots((mask,), False, 0, capacity)
                add_selected((mask,), False)

    whole = squares[0]
    for mask in range(1, n):
        square_copy(mask).wait_recv()
        whole = whole + squares[mask]
    for tile in range(tiles_here):
        norm[:, pl.ds(tile * TILE, TILE)] = jnp.sqrt(whole[tile : tile + 1])
    for load in loads:
        load.wait()
    for copy in started:
        copy.wait_send()
    for mask in range(1, n):
        square_copy(mask).wait_send()


def update_kernel(late_count, group, *refs):
    held_a, held_g = refs[:late_count], refs[late_count : 2 * late_count]
    refs = refs[2 * late_count :]
    sel_states, (off_moment, off_second) = refs[:3], refs[3:5]
    total, sel_sum, norm, weight_source = refs[5:9]
    table_source = refs[9]
    sel_new, off_new, norm_new = refs[10:13], refs[13:16], refs[16]
    table, weights, stage, sel_stage, load_sem, stage_sem, sel_sem = refs[17:]
    me = lax.axis_index("dp")
    capacity, row_block = total.shape[:2]
    sel_count = sel_sum.shape[1] // TILE
    groups = capacity // group
    depth = weights.shape[0]
    rows_once = min(ROWS_ONCE, row_block)

    def load_of(at, ring):
        return pltpu.make_async_copy(
            weight_source.at[pl.ds(at * group, group)], weights.at[ring], load_sem.at[ring]
        )

    def out_of(which, at, ring):
        return pltpu.make_async_copy(
            stage.at[which, ring],
            off_new[which].at[pl.ds(at * group, group)],
            stage_sem.at[which, ring],
        )

    table_copy = pltpu.make_async_copy(table_source, table, sel_sem.at[4])
    table_copy.start()
    for at in range(min(depth, groups)):
        load_of(at, at).start()
    norm_copy = pltpu.make_async_copy(norm.at[0], norm_new, sel_sem.at[3])
    norm_copy.start()
    table_copy.wait()

    for i in range(sel_count):
        tile, place = table[3 * capacity + i], pl.ds(i * TILE, TILE)
        for row in range(0, row_block, rows_once):
            rows = pl.ds(row, rows_once)
            grad = sel_sum[rows, place]
            for a, g in zip(held_a, held_g):
                grad = grad + jnp.dot(
                    a[me, rows], g[tile], preferred_element_type=jnp.float32
                )
            news = adam_update(*(state[rows, place] for state in sel_states), grad)
            for which in range(3):
                sel_stage[which, rows, place] = news[which]
    sel_copies = [
        pltpu.make_async_copy(sel_stage.at[which], sel_new[which], sel_sem.at[which])
        for which in range(3)
    ]
    for copy in sel_copies:
        copy.start()

    @pl.loop(0, groups)
    def _(at):
        ring, turn = lax.rem(at, depth), lax.rem(at, 2)
        load_of(at, ring).wait()

        @pl.when(at >= 2)
        def _():
            for which in range(3):
                out_of(which, at, turn).wait()

        for k in range(group):
            slot = at * group + k
            block, tile = table[capacity + slot], table[slot]
            full = table[2 * capacity + slot] > 0
            for row in range(0, row_block, rows_once):
                rows = pl.ds(row, rows_once)
                value = total[slot, rows]
                for a, g in zip(held_a, held_g):
                    value = value + rounded(
                        jnp.dot(
                            a[block, rows], g[tile], preferred_element_type=jnp.float32
                        )
                    )
                grad = jnp.where(full, rounded(value), 0.0)
                news = adam_update(
                    weights[ring, k, rows],
                    off_moment[slot, rows],
                    off_second[slot, rows],
                    grad,
                )
                for which in range(3):
                    stage[which, turn, k, rows] = news[which]
        for which in range(3):
            out_of(which, at, turn).start()

        @pl.when(at + depth < groups)
        def _():
            load_of(at + depth, ring).start()

    for at in range(max(groups - 2, 0), groups):
        for which in range(3):
            out_of(which, at, at % 2).wait()
    for copy in sel_copies:
        copy.wait()
    norm_copy.wait()


def body(
    acts,
    grad_out,
    selected,
    owner,
    sel_weight,
    sel_moment,
    sel_second,
    off_weight,
    off_moment,
    off_second,
):
    n = lax.axis_size("dp")
    tokens_here, rows_all = acts.shape
    cols_here = grad_out.shape[1]
    tiles_here = cols_here // TILE
    sel_count = selected.shape[1]
    row_block = rows_all // n
    capacity = off_weight.shape[2]
    piece_count = owner.shape[1]
    paired = n == 8 and lax.axis_size("tensor") % 2 == 0
    late = (6, 7) if paired else (n - 1,)
    sel_states = (sel_weight, sel_moment, sel_second)
    slot_shape = (capacity, row_block, TILE)
    off_states = tuple(
        state.reshape(slot_shape) for state in (off_weight, off_moment, off_second)
    )
    in_vmem = pl.BlockSpec(memory_space=pltpu.VMEM)
    in_smem = pl.BlockSpec(memory_space=pltpu.SMEM)
    anywhere = pl.BlockSpec(memory_space=pltpu.HBM)
    a_shape, g_shape = (n, row_block, tokens_here), (tiles_here, tokens_here, TILE)
    table_shape = (3 * capacity + sel_count,)
    sel_shape = (row_block, sel_count * TILE)
    sends = 42 if paired else 2 * (n - 1)
    early_count = n - len(late)
    sel_row = selected.reshape(sel_count)
    half = jnp.dtype(jnp.bfloat16).itemsize
    gathered = (early_count + 1) * tokens_here * rows_all + early_count * tokens_here * cols_here
    gather_limit = half * gathered + 3 * MIB
    update_limit = gather_limit
    table = pl.pallas_call(
        functools.partial(table_kernel, n, capacity),
        name="tables",
        out_shape=jax.ShapeDtypeStruct(table_shape, jnp.int32),
        in_specs=[in_smem] * 2,
        out_specs=in_smem,
        scratch_shapes=[
            pltpu.SMEM((piece_count + 2,), jnp.int32),
            pltpu.SMEM((tiles_here + 1,), jnp.int32),
            pltpu.SMEM((tiles_here - sel_count,), jnp.int32),
        ],
    )(sel_row, owner.reshape(piece_count))
    outs = pl.pallas_call(
        functools.partial(gather_kernel, n, paired, late),
        name="gather",
        out_shape=[pltpu.VMEM(a_shape, jnp.bfloat16)] * len(late)
        + [pltpu.VMEM(g_shape, jnp.bfloat16)] * len(late)
        + [pltpu.VMEM(sel_shape, jnp.float32)] * 3
        + [pltpu.VMEM(slot_shape, jnp.float32)] * 2
        + [
            pltpu.VMEM(slot_shape, jnp.float32),
            pltpu.VMEM(sel_shape, jnp.float32),
            pltpu.VMEM((1, cols_here), jnp.float32),
        ],
        in_specs=[anywhere] * 8,
        out_specs=[in_vmem] * (2 * len(late) + 8),
        scratch_shapes=[
            pltpu.SMEM(table_shape, jnp.int32),
            pltpu.VMEM((tokens_here, rows_all), jnp.bfloat16),
            pltpu.VMEM((n, tiles_here, TILE), jnp.float32),
            pltpu.SemaphoreType.DMA((sends,)),
            pltpu.SemaphoreType.DMA((6 * (n - 1),)),
            pltpu.SemaphoreType.DMA((n - 1,)),
            pltpu.SemaphoreType.DMA((n - 1,)),
            pltpu.SemaphoreType.DMA((7,)),
            pltpu.SemaphoreType.DMA((tiles_here,)),
        ]
        + [pltpu.VMEM(a_shape, jnp.bfloat16)] * early_count
        + [pltpu.VMEM(g_shape, jnp.bfloat16)] * early_count,
        compiler_params=pltpu.CompilerParams(
            collective_id=0, has_side_effects=True, vmem_limit_bytes=gather_limit
        ),
    )(
        *(
            in_hbm(each)
            for each in (
                table,
                acts,
                grad_out,
                *sel_states,
                *off_states[1:],
            )
        )
    )
    lates, outs = outs[: 2 * len(late)], list(outs[2 * len(late) :])
    kept, (total, sel_sum, norm) = outs[:5], outs[5:]
    group = unroll_of(capacity)
    news = pl.pallas_call(
        functools.partial(update_kernel, len(late), group),
        name="update",
        out_shape=[jax.ShapeDtypeStruct(sel_shape, jnp.float32)] * 3
        + [jax.ShapeDtypeStruct(slot_shape, jnp.float32)] * 3
        + [jax.ShapeDtypeStruct((cols_here,), jnp.float32)],
        in_specs=[in_vmem] * (2 * len(late) + 8) + [anywhere] * 2,
        out_specs=[anywhere] * 7,
        scratch_shapes=[
            pltpu.SMEM(table_shape, jnp.int32),
            pltpu.VMEM((DEPTH, group, row_block, TILE), jnp.float32),
            pltpu.VMEM((3, 2, group, row_block, TILE), jnp.float32),
            pltpu.VMEM((3, *sel_shape), jnp.float32),
            pltpu.SemaphoreType.DMA((DEPTH,)),
            pltpu.SemaphoreType.DMA((3, 2)),
            pltpu.SemaphoreType.DMA((5,)),
        ],
        compiler_params=pltpu.CompilerParams(vmem_limit_bytes=update_limit),
    )(
        *lates,
        *kept,
        total,
        sel_sum,
        norm,
        in_hbm(off_states[0]),
        in_hbm(table),
    )
    return (
        news[6],
        *news[:3],
        *(new.reshape(off_weight.shape) for new in news[3:6]),
    )


def solution(mesh):
    placed = (
        P("dp", None),
        P("dp", "tensor"),
        P("tensor", None),
        P("tensor", None, None),
        P("dp", "tensor"),
        P("dp", "tensor"),
        P("dp", "tensor"),
        P("dp", "tensor", None, None, None),
        P("dp", "tensor", None, None, None),
        P("dp", "tensor", None, None, None),
    )
    return jax.shard_map(
        body,
        mesh=mesh,
        in_specs=placed,
        out_specs=(
            P("tensor"),
            P("dp", "tensor"),
            P("dp", "tensor"),
            P("dp", "tensor"),
            P("dp", "tensor", None, None, None),
            P("dp", "tensor", None, None, None),
            P("dp", "tensor", None, None, None),
        ),
        check_vma=False,
    )
```

time: 111 us -> 78.9 us (0.71)
  other arithmetic: 29.2 us -> 0 us
  local copies, waits for them, and re-layouts: 5.11 us -> 0 us
  Pallas kernels: 76.1 us -> 78.1 us
    sub x3 -> x0, other arithmetic: 25.7 us -> none  [the longest x2 25.6 us: adam_update(): weight - learn_rate * (update + decay_rate * weight)]
    transpose x1 -> x0, local copies, waits for them, and re-layouts: 2.26 us -> none  [body(): acts_t = acts.T.reshape(n, row_block, tokens_here)]
    pallas_call x1 -> x3, Pallas kernels: 76.1 us -> 78.1 us  [the longest x1 57.5 us: body(): pl.pallas_call(functools.partial(gather_kernel, n, paired, late), name='g...]
    unnamed x11 -> x0, local copies, waits for them, and re-layouts: 1.58 us -> none
    reshape x1 -> x0, local copies, waits for them, and re-layouts: 1.28 us -> none  [body(): grad_out.reshape(tokens_here, tiles_here, TILE)]
where the time goes in v1:
time: 78.9 us; the launch traced here: 78.7 us
  Pallas kernels  78.1 us (99%)
    pallas_call x1, Pallas kernels, body(): pl.pallas_call(functools.partial(gather_kernel, n, paired, late), name='g...  57.5 us
    pallas_call x1, Pallas kernels, body(): pl.pallas_call(functools.partial(update_kernel, len(late), group), name='...  16.9 us
    pallas_call x1, Pallas kernels, body(): pl.pallas_call(functools.partial(table_kernel, n, capacity), name='tables...  3.67 us

profile of v1, /device:TPU:0, one launch (start us, length us, event | category | flops | bytes accessed | tf_op | source)
XLA Modules:
  0.0 78.7 jit_solution(12183944689737055866)
XLA Ops:
  0.6 3.7 %tables.1.table_source.refs_13_ = s32[112]{0:T(128)} custom-call(s32[4]{0:T(128)} %bitcast.12, s32[192]{0:T(256)} %bitcast.11), custom_call_target="tpu_custom_call" | custom-call | tf_op jit(solution)/shard_map/tables/pallas_call | solution.py:512
  4.3 57.5 %gather.1 = (bf16[8,512,128]{2,1,0:T(8,128)(2,1)S(1)}, bf16[8,512,128]{2,1,0:T(8,128)(2,1)S(1)}, bf16[28,128,128]{2,1,0:T(8,128)(2,1)S(1)}, bf16[28,128,128]{2,1...) custom-call(s32[112]{0:T(128)} %tables.1.table_source.refs_13_, ...), custom_call_target="tpu_custom_call" | custom-call | tf_op jit(solution)/shard_map/gather/pallas_call | solution.py:524
  61.8 16.9 %update.1 = (f32[512,512]{1,0:T(8,128)}, f32[512,512]{1,0:T(8,128)}, f32[512,512]{1,0:T(8,128)}, f32[36,512,128]{2,1,0:T(8,128)}, f32[36,512,128]{2,1,0:T(8,128)...) custom-call(bf16[8,512,128]{2,1,0:T(8,128)(2,1)S(1)} %get-tuple-element.26.refs_0_, ...), custom_call_target="tpu_custom_call" | custom-call | tf_op jit(solution)/shard_map/update/pallas_call | solution.py:569

commit v2 on v1

--- a/solution.py
+++ b/solution.py
@@ -8,7 +8,6 @@
 from jax.sharding import PartitionSpec as P
 
 TILE = 128
-DEPTH = 4
 ROWS_ONCE = 128
 MIB = 1024 * 1024
 
@@ -24,11 +23,13 @@
 
 def adam_update(weight, moment, second, grad):
     first_fix = 1.0 - beta_one**step_count
-    second_fix = 1.0 - beta_two**step_count
+    root_fix = (1.0 - beta_two**step_count) ** 0.5
     moment_new = beta_one * moment + (1.0 - beta_one) * grad
     second_new = beta_two * second + (1.0 - beta_two) * (grad * grad)
-    scale = jnp.sqrt(second_new * (1.0 / second_fix)) + adam_eps
-    update = moment_new * (learn_rate / first_fix) / scale
+    inverse = lax.rsqrt(second_new)
+    scale = second_new * inverse + adam_eps * root_fix
+    inverse = inverse + inverse * (1.0 - scale * inverse)
+    update = moment_new * (learn_rate * root_fix / first_fix) * inverse
     return weight * (1.0 - learn_rate * decay_rate) - update, moment_new, second_new
 
 
@@ -53,7 +54,7 @@
     return next(k for k in (3, 2, 1) if count % k == 0)
 
 
-def table_kernel(
+def make_tables(
     n, capacity, sel_tile, owner, table, next_piece, next_free, rest_tile
 ):
     me = lax.axis_index("dp")
@@ -103,18 +104,18 @@
         table[3 * capacity + k] = sel_tile[k]
 
 
-def gather_kernel(n, paired, late, table_source, acts, grad, *refs):
-    states, refs = refs[:5], refs[5:]
+def gather_kernel(n, paired, late, selected, owners, acts, grad, *refs):
+    states, refs = refs[:6], refs[6:]
     late_a, late_g = refs[: len(late)], refs[len(late) : 2 * len(late)]
     refs = refs[2 * len(late) :]
-    kept = refs[:5]
-    total, sel_sum, norm = refs[5:8]
+    kept = refs[:6]
+    total, sel_sum, norm, table = refs[6:10]
     early = [mask for mask in range(n) if mask not in late]
-    refs = refs[8:]
-    table, raw, squares = refs[:3]
-    send_sem, recv_sem, send_q, recv_q, load_sem, grad_sem = refs[3:9]
-    held_a = dict(zip(early, refs[9 : 9 + len(early)])) | dict(zip(late, late_a))
-    held_g = dict(zip(early, refs[9 + len(early) :])) | dict(zip(late, late_g))
+    refs = refs[10:]
+    raw, squares, sel_tile, owner, next_piece, next_free, rest_tile = refs[:7]
+    send_sem, recv_sem, send_q, recv_q, load_sem, grad_sem = refs[7:13]
+    held_a = dict(zip(early, refs[13 : 13 + len(early)])) | dict(zip(late, late_a))
+    held_g = dict(zip(early, refs[13 + len(early) :])) | dict(zip(late, late_g))
 
     layer = lax.axis_index("tensor")
     me = lax.axis_index("dp")
@@ -141,7 +142,11 @@
         }
 
     own_acts = pltpu.make_async_copy(acts, raw, load_sem.at[0])
-    own_table = pltpu.make_async_copy(table_source, table, load_sem.at[1])
+    own_tables = [pltpu.make_async_copy(owners, owner, load_sem.at[1])]
+    if sel_count == 1:
+        sel_tile[0] = selected[0]
+    else:
+        own_tables.append(pltpu.make_async_copy(selected, sel_tile, load_sem.at[2]))
     own_grads = [
         pltpu.make_async_copy(
             grad.at[:, pl.ds(tile * TILE, TILE)], held_g[0].at[tile], grad_sem.at[tile]
@@ -149,12 +154,14 @@
         for tile in range(tiles_here)
     ]
     own_acts.start()
-    own_table.start()
+    for copy in own_tables:
+        copy.start()
     for copy in own_grads:
         copy.start()
     loads = []
     for number, (source, target) in enumerate(zip(states, kept)):
-        load = pltpu.make_async_copy(source, target, load_sem.at[2 + number])
+        source = source.at[pl.ds(0, target.shape[0])]
+        load = pltpu.make_async_copy(source, target, load_sem.at[3 + number])
         loads.append(load)
 
     barrier = pltpu.get_barrier_semaphore()
@@ -171,7 +178,6 @@
         held_a[0][block] = raw[:, pl.ds(block * row_block, row_block)].T
     for copy in own_grads:
         copy.wait()
-    own_table.wait()
     pl.semaphore_wait(barrier, n if paired else n - 1)
 
     started = []
@@ -292,6 +298,9 @@
             send(kind, 0, core)
         for load in loads:
             load.start()
+        for copy in own_tables:
+            copy.wait()
+        make_tables(n, capacity, sel_tile, owner, table, next_piece, next_free, rest_tile)
         square_columns()
         for mask in range(1, n):
             square_copy(mask).start()
@@ -343,6 +352,9 @@
                 send(kind, 0, mask)
         for load in loads:
             load.start()
+        for copy in own_tables:
+            copy.wait()
+        make_tables(n, capacity, sel_tile, owner, table, next_piece, next_free, rest_tile)
         square_columns()
         for mask in range(1, n):
             square_copy(mask).start()
@@ -371,22 +383,20 @@
 def update_kernel(late_count, group, *refs):
     held_a, held_g = refs[:late_count], refs[late_count : 2 * late_count]
     refs = refs[2 * late_count :]
-    sel_states, (off_moment, off_second) = refs[:3], refs[3:5]
-    total, sel_sum, norm, weight_source = refs[5:9]
-    table_source = refs[9]
-    sel_new, off_new, norm_new = refs[10:13], refs[13:16], refs[16]
-    table, weights, stage, sel_stage, load_sem, stage_sem, sel_sem = refs[17:]
+    sel_states, (off_moment, off_second, ready) = refs[:3], refs[3:6]
+    total, sel_sum, norm, weight_source, table = refs[6:11]
+    sel_new, off_new, norm_new = refs[11:14], refs[14:17], refs[17]
+    later, stage, sel_stage, load_sem, stage_sem, sel_sem = refs[18:]
     me = lax.axis_index("dp")
     capacity, row_block = total.shape[:2]
     sel_count = sel_sum.shape[1] // TILE
     groups = capacity // group
-    depth = weights.shape[0]
+    begun = ready.shape[0] // group
     rows_once = min(ROWS_ONCE, row_block)
 
-    def load_of(at, ring):
-        return pltpu.make_async_copy(
-            weight_source.at[pl.ds(at * group, group)], weights.at[ring], load_sem.at[ring]
-        )
+    load = pltpu.make_async_copy(
+        weight_source.at[pl.ds(begun * group, later.shape[0])], later, load_sem.at[0]
+    )
 
     def out_of(which, at, ring):
         return pltpu.make_async_copy(
@@ -395,13 +405,9 @@
             stage_sem.at[which, ring],
         )
 
-    table_copy = pltpu.make_async_copy(table_source, table, sel_sem.at[4])
-    table_copy.start()
-    for at in range(min(depth, groups)):
-        load_of(at, at).start()
+    load.start()
     norm_copy = pltpu.make_async_copy(norm.at[0], norm_new, sel_sem.at[3])
     norm_copy.start()
-    table_copy.wait()
 
     for i in range(sel_count):
         tile, place = table[3 * capacity + i], pl.ds(i * TILE, TILE)
@@ -422,10 +428,8 @@
     for copy in sel_copies:
         copy.start()
 
-    @pl.loop(0, groups)
-    def _(at):
-        ring, turn = lax.rem(at, depth), lax.rem(at, 2)
-        load_of(at, ring).wait()
+    def update_group(at, weights, shift):
+        turn = lax.rem(at, 2)
 
         @pl.when(at >= 2)
         def _():
@@ -447,7 +451,7 @@
                     )
                 grad = jnp.where(full, rounded(value), 0.0)
                 news = adam_update(
-                    weights[ring, k, rows],
+                    weights[slot - shift, rows],
                     off_moment[slot, rows],
                     off_second[slot, rows],
                     grad,
@@ -457,9 +461,15 @@
         for which in range(3):
             out_of(which, at, turn).start()
 
-        @pl.when(at + depth < groups)
-        def _():
-            load_of(at + depth, ring).start()
+    @pl.loop(0, begun)
+    def _(at):
+        update_group(at, ready, 0)
+
+    load.wait()
+
+    @pl.loop(begun, groups)
+    def _(at):
+        update_group(at, later, begun * group)
 
     for at in range(max(groups - 2, 0), groups):
         for which in range(3):
@@ -505,22 +515,12 @@
     sends = 42 if paired else 2 * (n - 1)
     early_count = n - len(late)
     sel_row = selected.reshape(sel_count)
+    group = unroll_of(capacity)
+    ready = capacity // group * 2 // 3 * group
     half = jnp.dtype(jnp.bfloat16).itemsize
     gathered = (early_count + 1) * tokens_here * rows_all + early_count * tokens_here * cols_here
-    gather_limit = half * gathered + 3 * MIB
+    gather_limit = half * gathered + MIB // 2
     update_limit = gather_limit
-    table = pl.pallas_call(
-        functools.partial(table_kernel, n, capacity),
-        name="tables",
-        out_shape=jax.ShapeDtypeStruct(table_shape, jnp.int32),
-        in_specs=[in_smem] * 2,
-        out_specs=in_smem,
-        scratch_shapes=[
-            pltpu.SMEM((piece_count + 2,), jnp.int32),
-            pltpu.SMEM((tiles_here + 1,), jnp.int32),
-            pltpu.SMEM((tiles_here - sel_count,), jnp.int32),
-        ],
-    )(sel_row, owner.reshape(piece_count))
     outs = pl.pallas_call(
         functools.partial(gather_kernel, n, paired, late),
         name="gather",
@@ -529,21 +529,27 @@
         + [pltpu.VMEM(sel_shape, jnp.float32)] * 3
         + [pltpu.VMEM(slot_shape, jnp.float32)] * 2
         + [
+            pltpu.VMEM((ready, row_block, TILE), jnp.float32),
             pltpu.VMEM(slot_shape, jnp.float32),
             pltpu.VMEM(sel_shape, jnp.float32),
             pltpu.VMEM((1, cols_here), jnp.float32),
+            jax.ShapeDtypeStruct(table_shape, jnp.int32),
         ],
-        in_specs=[anywhere] * 8,
-        out_specs=[in_vmem] * (2 * len(late) + 8),
+        in_specs=[in_smem if sel_count == 1 else anywhere] + [anywhere] * 9,
+        out_specs=[in_vmem] * (2 * len(late) + 9) + [in_smem],
         scratch_shapes=[
-            pltpu.SMEM(table_shape, jnp.int32),
             pltpu.VMEM((tokens_here, rows_all), jnp.bfloat16),
             pltpu.VMEM((n, tiles_here, TILE), jnp.float32),
+            pltpu.SMEM((sel_count,), jnp.int32),
+            pltpu.SMEM((piece_count,), jnp.int32),
+            pltpu.SMEM((piece_count + 2,), jnp.int32),
+            pltpu.SMEM((tiles_here + 1,), jnp.int32),
+            pltpu.SMEM((tiles_here - sel_count,), jnp.int32),
             pltpu.SemaphoreType.DMA((sends,)),
             pltpu.SemaphoreType.DMA((6 * (n - 1),)),
             pltpu.SemaphoreType.DMA((n - 1,)),
             pltpu.SemaphoreType.DMA((n - 1,)),
-            pltpu.SemaphoreType.DMA((7,)),
+            pltpu.SemaphoreType.DMA((9,)),
             pltpu.SemaphoreType.DMA((tiles_here,)),
         ]
         + [pltpu.VMEM(a_shape, jnp.bfloat16)] * early_count
@@ -552,36 +558,36 @@
             collective_id=0, has_side_effects=True, vmem_limit_bytes=gather_limit
         ),
     )(
+        sel_row if sel_count == 1 else in_hbm(sel_row),
         *(
             in_hbm(each)
             for each in (
-                table,
+                owner.reshape(piece_count),
                 acts,
                 grad_out,
                 *sel_states,
                 *off_states[1:],
+                off_states[0],
             )
         )
     )
     lates, outs = outs[: 2 * len(late)], list(outs[2 * len(late) :])
-    kept, (total, sel_sum, norm) = outs[:5], outs[5:]
-    group = unroll_of(capacity)
+    kept, (total, sel_sum, norm, table) = outs[:6], outs[6:]
     news = pl.pallas_call(
         functools.partial(update_kernel, len(late), group),
         name="update",
         out_shape=[jax.ShapeDtypeStruct(sel_shape, jnp.float32)] * 3
         + [jax.ShapeDtypeStruct(slot_shape, jnp.float32)] * 3
         + [jax.ShapeDtypeStruct((cols_here,), jnp.float32)],
-        in_specs=[in_vmem] * (2 * len(late) + 8) + [anywhere] * 2,
+        in_specs=[in_vmem] * (2 * len(late) + 9) + [anywhere, in_smem],
         out_specs=[anywhere] * 7,
         scratch_shapes=[
-            pltpu.SMEM(table_shape, jnp.int32),
-            pltpu.VMEM((DEPTH, group, row_block, TILE), jnp.float32),
+            pltpu.VMEM((capacity - ready, row_block, TILE), jnp.float32),
             pltpu.VMEM((3, 2, group, row_block, TILE), jnp.float32),
             pltpu.VMEM((3, *sel_shape), jnp.float32),
-            pltpu.SemaphoreType.DMA((DEPTH,)),
+            pltpu.SemaphoreType.DMA((1,)),
             pltpu.SemaphoreType.DMA((3, 2)),
-            pltpu.SemaphoreType.DMA((5,)),
+            pltpu.SemaphoreType.DMA((4,)),
         ],
         compiler_params=pltpu.CompilerParams(vmem_limit_bytes=update_limit),
     )(
@@ -591,7 +597,7 @@
         sel_sum,
         norm,
         in_hbm(off_states[0]),
-        in_hbm(table),
+        table,
     )
     return (
         news[6],

time: 78.9 us -> 74.6 us (0.946)
  Pallas kernels: 78.1 us -> 73.8 us
    pallas_call x1 -> x0, Pallas kernels: 3.67 us -> none  [body(): pl.pallas_call(functools.partial(table_kernel, n, capacity), name='tables...]
    pallas_call x1, Pallas kernels: 16.9 us -> 15.7 us  [body(): pl.pallas_call(functools.partial(update_kernel, len(late), group), name='...]
where the time goes in v2:
time: 74.6 us; the launch traced here: 74.5 us
  Pallas kernels  73.8 us (99%)
    pallas_call x1, Pallas kernels, body(): pl.pallas_call(functools.partial(gather_kernel, n, paired, late), name='g...  58.1 us
    pallas_call x1, Pallas kernels, body(): pl.pallas_call(functools.partial(update_kernel, len(late), group), name='...  15.7 us

profile of v2, /device:TPU:0, one launch (start us, length us, event | category | flops | bytes accessed | tf_op | source)
XLA Modules:
  0.0 74.5 jit_solution(12078428149075050034)
XLA Ops:
  0.6 58.1 %gather.1 = (bf16[8,512,128]{2,1,0:T(8,128)(2,1)S(1)}, bf16[8,512,128]{2,1,0:T(8,128)(2,1)S(1)}, bf16[28,128,128]{2,1,0:T(8,128)(2,1)S(1)}, bf16[28,128,128]{2,1...) custom-call(s32[4]{0:T(128)} %bitcast.13, ...), custom_call_target="tpu_custom_call" | custom-call | tf_op jit(solution)/shard_map/gather/pallas_call | solution.py:524
  58.7 15.7 %update.1 = (f32[512,512]{1,0:T(8,128)}, f32[512,512]{1,0:T(8,128)}, f32[512,512]{1,0:T(8,128)}, f32[36,512,128]{2,1,0:T(8,128)}, f32[36,512,128]{2,1,0:T(8,128)...) custom-call(bf16[8,512,128]{2,1,0:T(8,128)(2,1)S(1)} %get-tuple-element.28.refs_0_, ...), custom_call_target="tpu_custom_call" | custom-call | tf_op jit(solution)/shard_map/update/pallas_call | solution.py:576

commit v3 on v2

--- a/solution.py
+++ b/solution.py
@@ -123,16 +123,17 @@
     sel_count = sel_sum.shape[1] // TILE
     row_block = total.shape[1]
     tiles_here = grad.shape[1] // TILE
-    kinds = ("a0", "a1", "z0", "z1", "g0", "g1")
+    kinds = ("a0", "a1", "z0", "z1", "s0", "g0", "g1")
     if paired:
         side, part = layer % 2, n // 4
-        cut = tiles_here // 2
+        first, cut = tiles_here // 7, tiles_here // 2
         parts = {
             "a0": (held_a, (pl.ds(side * 2 * part, part),)),
             "a1": (held_a, (pl.ds(side * 2 * part + part, part),)),
             "z0": (held_a, (pl.ds((1 - side) * 2 * part, part),)),
             "z1": (held_a, (pl.ds((1 - side) * 2 * part + part, part),)),
-            "g0": (held_g, (pl.ds(0, cut),)),
+            "s0": (held_g, (pl.ds(0, first),)),
+            "g0": (held_g, (pl.ds(first, cut - first),)),
             "g1": (held_g, (pl.ds(cut, tiles_here - cut),)),
         }
     else:
@@ -173,9 +174,6 @@
         pl.semaphore_signal(
             barrier, inc=1, device_id={"tensor": flip_bits(layer, 1)}, device_id_type=MESH
         )
-    own_acts.wait()
-    for block in range(n):
-        held_a[0][block] = raw[:, pl.ds(block * row_block, row_block)].T
     for copy in own_grads:
         copy.wait()
     pl.semaphore_wait(barrier, n if paired else n - 1)
@@ -287,9 +285,17 @@
         arrived(kind, mask)
         send(kind, mask, 1)
 
+    def turn_acts():
+        own_acts.wait()
+        for block in range(n):
+            held_a[0][block] = raw[:, pl.ds(block * row_block, row_block)].T
+
     if paired:
         core, near, far = 1, 2, 4
         both = near ^ far
+        send("s0", 0, near)
+        send("s0", 0, far)
+        turn_acts()
         send("a1", 0, near)
         send("a0", 0, far)
         send("a0", 0, near)
@@ -298,12 +304,6 @@
             send(kind, 0, core)
         for load in loads:
             load.start()
-        for copy in own_tables:
-            copy.wait()
-        make_tables(n, capacity, sel_tile, owner, table, next_piece, next_free, rest_tile)
-        square_columns()
-        for mask in range(1, n):
-            square_copy(mask).start()
         relay("a0", far)
         send("a0", far, near)
         send_across("a0", far)
@@ -314,17 +314,26 @@
         send("g0", 0, far)
         send("g0", 0, near)
         send("g1", 0, far)
+        square_columns()
+        for mask in range(1, n):
+            square_copy(mask).start()
         relay("a0", near)
         send_across("a0", near)
         relay("a1", far)
         send_across("a1", far)
-        complete(core)
-        add_slots((0, core), True, 0, capacity)
-        add_selected((0, core), True)
+        for copy in own_tables:
+            copy.wait()
+        make_tables(n, capacity, sel_tile, owner, table, next_piece, next_free, rest_tile)
         relay("a0", both)
         send_across("a0", both)
         relay("a1", both)
         send_across("a1", both)
+        complete(core)
+        add_slots((0, core), True, 0, capacity)
+        add_selected((0, core), True)
+        relay("s0", far)
+        send("s0", far, near)
+        relay("s0", near)
         relay("z0", far)
         relay("z1", near)
         relay("z0", near)
@@ -343,10 +352,12 @@
         relay("z1", both)
         add_slots(middle, False, capacity // 2, capacity)
         add_selected(middle, False)
+        relay("s0", both)
         relay("g0", both)
         relay("g1", both)
         complete(both ^ core)
     else:
+        turn_acts()
         for mask in range(1, n):
             for kind in parts:
                 send(kind, 0, mask)
@@ -429,9 +440,9 @@
         copy.start()
 
     def update_group(at, weights, shift):
-        turn = lax.rem(at, 2)
-
-        @pl.when(at >= 2)
+        turn = lax.rem(at, 4)
+
+        @pl.when(at >= 4)
         def _():
             for which in range(3):
                 out_of(which, at, turn).wait()
@@ -471,9 +482,9 @@
     def _(at):
         update_group(at, later, begun * group)
 
-    for at in range(max(groups - 2, 0), groups):
+    for at in range(max(groups - 4, 0), groups):
         for which in range(3):
-            out_of(which, at, at % 2).wait()
+            out_of(which, at, at % 4).wait()
     for copy in sel_copies:
         copy.wait()
     norm_copy.wait()
@@ -512,10 +523,10 @@
     a_shape, g_shape = (n, row_block, tokens_here), (tiles_here, tokens_here, TILE)
     table_shape = (3 * capacity + sel_count,)
     sel_shape = (row_block, sel_count * TILE)
-    sends = 42 if paired else 2 * (n - 1)
+    sends = 49 if paired else 2 * (n - 1)
     early_count = n - len(late)
     sel_row = selected.reshape(sel_count)
-    group = unroll_of(capacity)
+    group = 2 if capacity % 2 == 0 else 1
     ready = capacity // group * 2 // 3 * group
     half = jnp.dtype(jnp.bfloat16).itemsize
     gathered = (early_count + 1) * tokens_here * rows_all + early_count * tokens_here * cols_here
@@ -546,7 +557,7 @@
             pltpu.SMEM((tiles_here + 1,), jnp.int32),
             pltpu.SMEM((tiles_here - sel_count,), jnp.int32),
             pltpu.SemaphoreType.DMA((sends,)),
-            pltpu.SemaphoreType.DMA((6 * (n - 1),)),
+            pltpu.SemaphoreType.DMA((7 * (n - 1),)),
             pltpu.SemaphoreType.DMA((n - 1,)),
             pltpu.SemaphoreType.DMA((n - 1,)),
             pltpu.SemaphoreType.DMA((9,)),
@@ -583,10 +594,10 @@
         out_specs=[anywhere] * 7,
         scratch_shapes=[
             pltpu.VMEM((capacity - ready, row_block, TILE), jnp.float32),
-            pltpu.VMEM((3, 2, group, row_block, TILE), jnp.float32),
+            pltpu.VMEM((3, 4, group, row_block, TILE), jnp.float32),
             pltpu.VMEM((3, *sel_shape), jnp.float32),
             pltpu.SemaphoreType.DMA((1,)),
-            pltpu.SemaphoreType.DMA((3, 2)),
+            pltpu.SemaphoreType.DMA((3, 4)),
             pltpu.SemaphoreType.DMA((4,)),
         ],
         compiler_params=pltpu.CompilerParams(vmem_limit_bytes=update_limit),

time: 74.6 us -> 72.3 us (0.969)
  Pallas kernels: 73.8 us -> 71.5 us
    pallas_call x1, Pallas kernels: 15.7 us -> 13.7 us  [body(): pl.pallas_call(functools.partial(update_kernel, len(late), group), name='...]
where the time goes in v3:
time: 72.3 us; the launch traced here: 72.1 us
  Pallas kernels  71.5 us (99%)
    pallas_call x1, Pallas kernels, body(): pl.pallas_call(functools.partial(gather_kernel, n, paired, late), name='g...  57.8 us
    pallas_call x1, Pallas kernels, body(): pl.pallas_call(functools.partial(update_kernel, len(late), group), name='...  13.7 us

profile of v3, /device:TPU:0, one launch (start us, length us, event | category | flops | bytes accessed | tf_op | source)
XLA Modules:
  0.0 72.1 jit_solution(3828678930341366803)
XLA Ops:
  0.6 57.8 %gather.1 = (bf16[8,512,128]{2,1,0:T(8,128)(2,1)S(1)}, bf16[8,512,128]{2,1,0:T(8,128)(2,1)S(1)}, bf16[28,128,128]{2,1,0:T(8,128)(2,1)S(1)}, bf16[28,128,128]{2,1...) custom-call(s32[4]{0:T(128)} %bitcast.13, ...), custom_call_target="tpu_custom_call" | custom-call | tf_op jit(solution)/shard_map/gather/pallas_call | solution.py:535
  58.4 13.7 %update.1 = (f32[512,512]{1,0:T(8,128)}, f32[512,512]{1,0:T(8,128)}, f32[512,512]{1,0:T(8,128)}, f32[36,512,128]{2,1,0:T(8,128)}, f32[36,512,128]{2,1,0:T(8,128)...) custom-call(bf16[8,512,128]{2,1,0:T(8,128)(2,1)S(1)} %get-tuple-element.28.refs_0_, ...), custom_call_target="tpu_custom_call" | custom-call | tf_op jit(solution)/shard_map/update/pallas_call | solution.py:587
